TPU v7x, 32 devices: a whole 2x2x4 slice. The times are simulated.
32 devices in a mesh: ta: 2 (over x), gx: 16 (over z, y, core).
Axes of the slice: x: 2, y: 2, z: 4, core: 2. Of those that a mesh axis runs over, the one named last changes fastest.
Arguments:
- voltages: bfloat16 [2, 128, 2, 256, 512], P('ta', 'gx'), may hold values from -6 to 6
- weights: bfloat16 [2, 256, 2, 512, 64], P(None, 'gx'), may hold values from -0.125 to 0.125
Outputs:
- spectra: float32 [256, 2, 512, 64], P(None, None, 'gx', 'ta')
All inputs are finite; a program needn't handle non-finite values.
Results may differ from a plain program's by a relative error of at most 0.0003.
Values may be sent and summed in bfloat16 or wider, within the bound.
A program may use at most 64 MiB of HBM per device.

v0:
```python
import functools

import jax
import jax.numpy as jnp
import numpy as np
from jax import lax
from jax.experimental import pallas as pl
from jax.experimental.pallas import tpu as pltpu
from jax.sharding import PartitionSpec as P

BF16 = np.dtype(jnp.bfloat16)
MESH = pl.DeviceIdType.MESH
CHUNKS = 4
PIECES = 4
LEAD = 2


def beam_power(voltage, weight_block):
    antennas = weight_block.shape[3]
    beam_count = weight_block.shape[2]
    powers = []
    for side_index in range(2):
        real_w = weight_block[side_index, 0]
        imag_w = weight_block[side_index, 1]
        upper_rows = jnp.stack([real_w, -imag_w], axis=-1).reshape(beam_count, 2 * antennas)
        bottom_half_rows = jnp.stack([imag_w, real_w], axis=-1).reshape(beam_count, 2 * antennas)
        matrix = jnp.concatenate([upper_rows, bottom_half_rows], 0)
        signal = voltage[side_index * antennas : (side_index + 1) * antennas].reshape(
            2 * antennas, -1
        )
        beam_voltage_field = jnp.dot(matrix, signal, preferred_element_type=jnp.float32)
        power = (
            beam_voltage_field[:beam_count] * beam_voltage_field[:beam_count]
            + beam_voltage_field[beam_count:] * beam_voltage_field[beam_count:]
        )
        powers.append(power.reshape(beam_count, -1, 8).sum(-1))
    return jnp.stack(powers, 0)


def channel_powers(turned, weights):

    def one_channel(column):
        voltage = lax.dynamic_index_in_dim(turned, column, 2, keepdims=False)
        weight_block = lax.dynamic_index_in_dim(weights, column, 1, keepdims=False)
        return beam_power(voltage, weight_block)

    return lax.map(one_channel, jnp.arange(turned.shape[2], dtype=jnp.int32))


def plain_on_device(voltages, weights):
    turned = lax.all_to_all(voltages, "gx", split_axis=3, concat_axis=1, tiled=True)
    partial_power_value = channel_powers(turned[0], weights)
    relaid = lax.all_to_all(partial_power_value, "gx", split_axis=2, concat_axis=0, tiled=True)
    return lax.psum_scatter(relaid, "ta", scatter_dimension=3, tiled=True)


def kernel(
    nx, ng, v_ref, w_hbm, turn_ref, mix_ref, gather_ref, out_ref,
    sbuf, vrecv, w_ref, pbuf,
    w_sem, wsend, wz, relay_sem, wx, vsend, vget, psend, pget,
):
    x = lax.axis_index("ta")
    g = lax.axis_index("gx")
    me = x * ng + g
    n = nx * ng
    rows = v_ref.shape[0] * v_ref.shape[1]
    chans = v_ref.shape[2] // ng
    half = v_ref.shape[3] // nx
    per = chans // CHUNKS
    group = ng // 2
    antennas2 = group * rows
    beams = w_ref.shape[4]
    side = g // group
    u = lax.rem(g, group)
    partner = lax.rem(g + group, ng)
    steps = 2 * CHUNKS
    dests = nx * group
    mine = x * group + u
    piece = chans // nx // PIECES

    w_copy = pltpu.make_async_copy(w_hbm.at[side], w_ref.at[0], w_sem)
    w_copy.start()

    barrier = pltpu.get_barrier_semaphore()

    def greet(i, _):
        d = lax.rem(me + i, n)
        pl.semaphore_signal(
            barrier, inc=1, device_id=(d // ng, lax.rem(d, ng)), device_id_type=MESH
        )
        return 0

    lax.fori_loop(1, n, greet, 0)

    def turn_side(which):
        base = lax.rem(which + side, 2) * CHUNKS

        def turn(i, _):
            start = pl.multiple_of((which * group + i) * chans, chans)
            block = v_ref[:, :, pl.ds(start, chans), :].reshape(rows * chans, nx * half)
            turned = jnp.dot(turn_ref[...], block, preferred_element_type=jnp.float32)
            turned = turned.astype(jnp.bfloat16).reshape(CHUNKS, per, rows, nx * half)
            for k in range(nx):
                sbuf[pl.ds(base, CHUNKS), k * group + i] = turned[
                    :, :, :, k * half : (k + 1) * half
                ]
            return 0

        lax.fori_loop(0, group, turn, 0)

    def send_voltages(k):
        pltpu.make_async_copy(sbuf.at[k, mine], vrecv.at[k, mine], vget.at[k]).start()

        def send(i, _):
            d = lax.rem(mine + i, dests)
            pltpu.make_async_remote_copy(
                src_ref=sbuf.at[k, d],
                dst_ref=vrecv.at[k, mine],
                send_sem=vsend.at[k],
                recv_sem=vget.at[k],
                device_id=(d // group, side * group + lax.rem(d, group)),
                device_id_type=MESH,
            ).start()
            return 0

        lax.fori_loop(1, dests, send, 0)

    def send_weights(i):
        span = pl.ds((x * PIECES + i) * piece, piece)
        pltpu.make_async_remote_copy(
            src_ref=w_hbm.at[1 - side, span],
            dst_ref=w_ref.at[1, span],
            send_sem=wsend,
            recv_sem=wz.at[i],
            device_id=(x, partner),
            device_id_type=MESH,
        ).start()

    def relay_weights(i):
        block = w_ref.at[1, pl.ds((x * PIECES + i) * piece, piece)]
        pltpu.make_async_copy(block, block, wz.at[i]).wait()
        pltpu.make_async_remote_copy(
            src_ref=block,
            dst_ref=block,
            send_sem=relay_sem,
            recv_sem=wx,
            device_id=(1 - x, g),
            device_id_type=MESH,
        ).start()

    turn_side(side)
    pl.semaphore_wait(barrier, n - 1)
    for k in range(LEAD):
        send_voltages(k)
        send_weights(k)
    turn_side(1 - side)
    w_copy.wait()

    def step(k, _):
        pltpu.make_async_copy(vrecv.at[k], vrecv.at[k], vget.at[k]).wait()

        @pl.when(k + LEAD < steps)
        def _():
            send_voltages(k + LEAD)

        @pl.when(k + LEAD < PIECES)
        def _():
            send_weights(k + LEAD)

        @pl.when((k >= 1) & (k <= PIECES))
        def _():
            relay_weights(k - 1)

        @pl.when(k == CHUNKS)
        def _():
            other = w_ref.at[1, pl.ds((1 - x) * PIECES * piece, PIECES * piece)]
            pltpu.make_async_copy(other, other, wx).wait()

        which = k // CHUNKS
        part_of = lax.rem(k, CHUNKS)

        def channel(c, _):
            w = w_ref[which, part_of * per + c].reshape(antennas2, beams).T
            power = None
            for h in range(nx):
                v = vrecv[k, h * group : (h + 1) * group, c].reshape(antennas2, half)
                mixed = jnp.dot(mix_ref[...], v, preferred_element_type=jnp.float32)
                mixed = mixed.astype(jnp.bfloat16)
                re = jnp.dot(w, mixed[:antennas2], preferred_element_type=jnp.float32)
                im = jnp.dot(w, mixed[antennas2:], preferred_element_type=jnp.float32)
                part = re * re + im * im
                power = part if power is None else power + part
            own = beams // ng
            packs = own // 8
            power = power.reshape(ng, packs, 8, half)
            total = None
            for m in range(packs):
                p = power[:, m].reshape(ng * 8, half)
                high = p.astype(jnp.bfloat16)
                low = (p - high.astype(jnp.float32)).astype(jnp.bfloat16)
                t = jnp.dot(high, gather_ref[m], preferred_element_type=jnp.float32)
                t += jnp.dot(low, gather_ref[m], preferred_element_type=jnp.float32)
                total = t if total is None else total + t
            pbuf[k, :, c] = total.reshape(ng, 8, 128)
            return 0

        lax.fori_loop(0, per, channel, 0)

        target = out_ref.at[side, lax.rem(g + which * group, ng), part_of]
        pltpu.make_async_copy(pbuf.at[k, g], target, pget).start()

        def send(i, _):
            d = lax.rem(g + i, ng)
            pltpu.make_async_remote_copy(
                src_ref=pbuf.at[k, d],
                dst_ref=target,
                send_sem=psend,
                recv_sem=pget,
                device_id=(x, d),
                device_id_type=MESH,
            ).start()
            return 0

        lax.fori_loop(1, ng, send, 0)
        return 0

    lax.fori_loop(0, steps, step, 0)

    pltpu.make_async_copy(out_ref, out_ref, pget).wait()
    for k in range(steps):
        sent = sbuf.at[k, pl.ds(0, dests - 1)]
        pltpu.make_async_copy(sent, sent, vsend.at[k]).wait()
    sent = pbuf.at[:, pl.ds(0, ng - 1)]
    pltpu.make_async_copy(sent, sent, psend).wait()
    sent = w_ref.at[1, pl.ds(0, PIECES * piece)]
    pltpu.make_async_copy(sent, sent, wsend).wait()
    pltpu.make_async_copy(sent, sent, relay_sem).wait()


def spread_kernel(in_ref, out_ref):
    channels, bins = out_ref.shape[3], out_ref.shape[2]
    for r in range(8):
        lanes = in_ref[0, pl.ds(r, channels, stride=8), :].T
        for m in range(128 // bins):
            out_ref[0, m * 8 + r] = lanes[m * bins : (m + 1) * bins]


def on_device(nx, ng, voltages, weights):
    v = voltages[0]
    streams, parts, channels, samples = v.shape
    rows, chans, half = streams * parts, channels // ng, samples // nx
    per = chans // CHUNKS
    group = ng // 2
    antennas = group * streams
    beams = weights.shape[3]
    own = beams // ng
    packs = own // 8
    bins = half // 8

    i = np.arange(rows * chans)[:, None]
    j = np.arange(rows * chans)[None, :]
    turn = ((j % chans == i // rows) & (j // chans == i % rows)).astype(BF16)
    i = np.arange(4 * antennas)[:, None]
    j = np.arange(2 * antennas)[None, :]
    block = i // antennas
    wants = 2 * (i % antennas) + np.where((block == 0) | (block == 3), 0, 1)
    mix = np.where(j == wants, np.where(block == 1, -1.0, 1.0), 0.0).astype(BF16)
    m = np.arange(packs)[:, None, None]
    s = np.arange(half)[None, :, None]
    lane = np.arange(128)[None, None, :]
    gather = (lane == m * bins + s // 8).astype(BF16)

    turned_weights = jnp.swapaxes(weights, 3, 4)
    vmem = pl.BlockSpec(memory_space=pltpu.VMEM)
    anywhere = pl.BlockSpec(memory_space=pl.ANY)
    packed = pl.pallas_call(
        functools.partial(kernel, nx, ng),
        out_shape=jax.ShapeDtypeStruct((2, ng, CHUNKS, per, 8, 128), jnp.float32),
        in_specs=[vmem, anywhere, vmem, vmem, vmem],
        out_specs=anywhere,
        scratch_shapes=[
            pltpu.VMEM((2 * CHUNKS, nx * group, per, rows, half), jnp.bfloat16),
            pltpu.VMEM((2 * CHUNKS, nx * group, per, rows, half), jnp.bfloat16),
            pltpu.VMEM(turned_weights.shape, jnp.bfloat16),
            pltpu.VMEM((2 * CHUNKS, ng, per, 8, 128), jnp.float32),
            pltpu.SemaphoreType.DMA,
            pltpu.SemaphoreType.DMA,
            pltpu.SemaphoreType.DMA((PIECES,)),
            pltpu.SemaphoreType.DMA,
            pltpu.SemaphoreType.DMA,
            pltpu.SemaphoreType.DMA((2 * CHUNKS,)),
            pltpu.SemaphoreType.DMA((2 * CHUNKS,)),
            pltpu.SemaphoreType.DMA,
            pltpu.SemaphoreType.DMA,
        ],
        compiler_params=pltpu.CompilerParams(
            collective_id=0, has_side_effects=True, vmem_limit_bytes=56 * 1024 * 1024
        ),
    )(v, turned_weights, turn, mix, gather)

    spread = pl.pallas_call(
        spread_kernel,
        grid=(2,),
        out_shape=jax.ShapeDtypeStruct((2, own, bins, channels), jnp.float32),
        in_specs=[pl.BlockSpec((1, channels * 8, 128), lambda q: (q, 0, 0))],
        out_specs=pl.BlockSpec((1, own, bins, channels), lambda q: (q, 0, 0, 0)),
    )(packed.reshape(2, channels * 8, 128))
    return spread.transpose(3, 0, 1, 2)


def solution(mesh):
    nx, ng = mesh.shape["ta"], mesh.shape["gx"]

    def body(voltages, weights):
        _, streams, parts, channels, samples = voltages.shape
        rows, chans, half = streams * parts, channels // ng, samples // nx
        own = weights.shape[3] // ng
        fits = (
            nx == 2
            and rows % 16 == 0
            and chans % 16 == 0
            and half % 128 == 0
            and own % 8 == 0
            and (own // 8) * (half // 8) == 128
        )
        if fits:
            return on_device(nx, ng, voltages, weights)
        return plain_on_device(voltages, weights)

    in_specs = (P("ta", "gx", None, None, None), P(None, "gx", None, None, None))
    out_specs = P(None, None, "gx", "ta")
    return jax.shard_map(
        body, mesh=mesh, in_specs=in_specs, out_specs=out_specs, check_vma=False
    )
```

profile of v0, /device:TPU:25, one launch (start us, length us, event | category | flops | bytes accessed | tf_op | source)
XLA Modules:
  0.0 119.8 jit_solution(2674309838933829367)
XLA Ops:
  0.0 116.9 %shard_map.55 = f32[2,16,4,4,8,128]{5,4,3,2,1,0:T(8,128)} custom-call(bf16[8,2,256,512]{3,2,1,0:T(8,128)(2,1)} %bitcast.5, bf16[2,16,2,64,512]{4,3,2,1,0:T(8,128)(2,1)} %bitcast.6, bf16[256,256]{1,0:T(8,128)(2,1)} %constant.6.clone.turn_ref, bf16[256,128]{1,0:T(8,128)(2,1)} %constant.7.clone.mix_ref, bf16[4,256,128]{2,1,0:T(8,128)(2,1)} %constant.8.clone.gather_ref), custom_call_target="tpu_custom_call" | custom-call | tf_op jit(solution)/shard_map/pallas_call | solution.py:276
  116.9 2.9 %shard_map.56 = f32[2,32,32,256]{3,2,1,0:T(8,128)} custom-call(f32[2,2048,128]{2,1,0:T(8,128)} %bitcast.4), custom_call_target="tpu_custom_call" | custom-call | tf_op jit(solution)/shard_map/pallas_call | solution.py:301
where the time goes:
time: 120 us
  Pallas kernels  120 us (100%)
    pallas_call x1, Pallas kernels, on_device(): pl.pallas_call(functools.partial(kernel, nx, ng), out_shape=jax.ShapeDtyp...  117 us
    pallas_call x1, Pallas kernels, on_device(): pl.pallas_call(spread_kernel, grid=(2,), out_shape=jax.ShapeDtypeStruct((...  2.9 us

commit v1 on v0

--- a/solution.py
+++ b/solution.py
@@ -13,6 +13,8 @@
 CHUNKS = 4
 PIECES = 4
 LEAD = 2
+TOP = 2.0**15.75
+FLOOR = 2.0**-90
 
 
 def beam_power(voltage, weight_block):
@@ -55,9 +57,9 @@
 
 
 def kernel(
-    nx, ng, v_ref, w_hbm, turn_ref, mix_ref, gather_ref, out_ref,
-    sbuf, vrecv, w_ref, pbuf,
-    w_sem, wsend, wz, relay_sem, wx, vsend, vget, psend, pget,
+    nx, ng, v_ref, w_hbm, turn_ref, mix_ref, gather_ref, out_ref, peak_ref,
+    sbuf, vrecv, w_ref, work, pbuf, peaks,
+    w_sem, wsend, wz, relay_sem, wx, vsend, vget, psend, pget, msend, mget,
 ):
     x = lax.axis_index("ta")
     g = lax.axis_index("gx")
@@ -179,7 +181,7 @@
         which = k // CHUNKS
         part_of = lax.rem(k, CHUNKS)
 
-        def channel(c, _):
+        def channel(c, peak):
             w = w_ref[which, part_of * per + c].reshape(antennas2, beams).T
             power = None
             for h in range(nx):
@@ -201,10 +203,22 @@
                 t = jnp.dot(high, gather_ref[m], preferred_element_type=jnp.float32)
                 t += jnp.dot(low, gather_ref[m], preferred_element_type=jnp.float32)
                 total = t if total is None else total + t
-            pbuf[k, :, c] = total.reshape(ng, 8, 128)
-            return 0
-
-        lax.fori_loop(0, per, channel, 0)
+            total = total.reshape(ng, 8, 128)
+            work[:, pl.ds(c, 1)] = total[:, None]
+            return jnp.maximum(peak, jnp.max(total, axis=0))
+
+        peak = lax.fori_loop(0, per, channel, jnp.zeros((8, 128), jnp.float32))
+        peak = jnp.maximum(jnp.max(peak, keepdims=True), FLOOR)
+        code = work[...].reshape(ng, per * 8, 128) * (TOP / peak)[None]
+        code = code * code
+        code = code * code
+        pbuf[k] = (code * code).astype(jnp.bfloat16)
+        row = lax.broadcasted_iota(jnp.int32, peaks.shape, 0)
+        lane = lax.broadcasted_iota(jnp.int32, peaks.shape, 1)
+        own_row = lax.rem(side + which, 2)
+        first = u * chans + part_of * per
+        held = (row == own_row) & (lane >= first) & (lane < first + per)
+        peaks[...] = jnp.where(held, peak, peaks[...])
 
         target = out_ref.at[side, lax.rem(g + which * group, ng), part_of]
         pltpu.make_async_copy(pbuf.at[k, g], target, pget).start()
@@ -224,23 +238,47 @@
         lax.fori_loop(1, ng, send, 0)
         return 0
 
+    peaks[...] = jnp.zeros_like(peaks)
     lax.fori_loop(0, steps, step, 0)
 
+    pltpu.make_async_copy(peaks, peak_ref.at[side, u], mget).start()
+
+    def send_peaks(i, _):
+        pltpu.make_async_remote_copy(
+            src_ref=peaks,
+            dst_ref=peak_ref.at[side, u],
+            send_sem=msend,
+            recv_sem=mget,
+            device_id=(x, lax.rem(g + i, ng)),
+            device_id_type=MESH,
+        ).start()
+        return 0
+
+    lax.fori_loop(1, ng, send_peaks, 0)
+
+    pltpu.make_async_copy(peak_ref, peak_ref, mget).wait()
     pltpu.make_async_copy(out_ref, out_ref, pget).wait()
     for k in range(steps):
         sent = sbuf.at[k, pl.ds(0, dests - 1)]
         pltpu.make_async_copy(sent, sent, vsend.at[k]).wait()
     sent = pbuf.at[:, pl.ds(0, ng - 1)]
     pltpu.make_async_copy(sent, sent, psend).wait()
+    sent = peak_ref.at[:, pl.ds(0, group - 1)]
+    pltpu.make_async_copy(sent, sent, msend).wait()
+    sent = peak_ref.at[0, pl.ds(0, 1)]
+    pltpu.make_async_copy(sent, sent, msend).wait()
     sent = w_ref.at[1, pl.ds(0, PIECES * piece)]
     pltpu.make_async_copy(sent, sent, wsend).wait()
     pltpu.make_async_copy(sent, sent, relay_sem).wait()
 
 
-def spread_kernel(in_ref, out_ref):
+def spread_kernel(in_ref, peak_ref, out_ref, power):
     channels, bins = out_ref.shape[3], out_ref.shape[2]
+    scale = jnp.sum(peak_ref[0], axis=0) * (1.0 / TOP)
+    scale = jnp.concatenate([scale[0:1], scale[1:2]], axis=1)
+    power[...] = jnp.exp(jnp.log(in_ref[0].astype(jnp.float32)) * 0.125)
     for r in range(8):
-        lanes = in_ref[0, pl.ds(r, channels, stride=8), :].T
+        lanes = power[pl.ds(r, channels, stride=8), :].T * scale
         for m in range(128 // bins):
             out_ref[0, m * 8 + r] = lanes[m * bins : (m + 1) * bins]
 
@@ -273,16 +311,21 @@
     turned_weights = jnp.swapaxes(weights, 3, 4)
     vmem = pl.BlockSpec(memory_space=pltpu.VMEM)
     anywhere = pl.BlockSpec(memory_space=pl.ANY)
-    packed = pl.pallas_call(
+    packed, peaks = pl.pallas_call(
         functools.partial(kernel, nx, ng),
-        out_shape=jax.ShapeDtypeStruct((2, ng, CHUNKS, per, 8, 128), jnp.float32),
+        out_shape=(
+            jax.ShapeDtypeStruct((2, ng, CHUNKS, per * 8, 128), jnp.bfloat16),
+            jax.ShapeDtypeStruct((2, group, 2, 128), jnp.float32),
+        ),
         in_specs=[vmem, anywhere, vmem, vmem, vmem],
-        out_specs=anywhere,
+        out_specs=(anywhere, anywhere),
         scratch_shapes=[
             pltpu.VMEM((2 * CHUNKS, nx * group, per, rows, half), jnp.bfloat16),
             pltpu.VMEM((2 * CHUNKS, nx * group, per, rows, half), jnp.bfloat16),
             pltpu.VMEM(turned_weights.shape, jnp.bfloat16),
-            pltpu.VMEM((2 * CHUNKS, ng, per, 8, 128), jnp.float32),
+            pltpu.VMEM((ng, per, 8, 128), jnp.float32),
+            pltpu.VMEM((2 * CHUNKS, ng, per * 8, 128), jnp.bfloat16),
+            pltpu.VMEM((2, 128), jnp.float32),
             pltpu.SemaphoreType.DMA,
             pltpu.SemaphoreType.DMA,
             pltpu.SemaphoreType.DMA((PIECES,)),
@@ -290,6 +333,8 @@
             pltpu.SemaphoreType.DMA,
             pltpu.SemaphoreType.DMA((2 * CHUNKS,)),
             pltpu.SemaphoreType.DMA((2 * CHUNKS,)),
+            pltpu.SemaphoreType.DMA,
+            pltpu.SemaphoreType.DMA,
             pltpu.SemaphoreType.DMA,
             pltpu.SemaphoreType.DMA,
         ],
@@ -302,9 +347,13 @@
         spread_kernel,
         grid=(2,),
         out_shape=jax.ShapeDtypeStruct((2, own, bins, channels), jnp.float32),
-        in_specs=[pl.BlockSpec((1, channels * 8, 128), lambda q: (q, 0, 0))],
+        in_specs=[
+            pl.BlockSpec((1, channels * 8, 128), lambda q: (q, 0, 0)),
+            pl.BlockSpec((1, group, 2, 128), lambda q: (q, 0, 0, 0)),
+        ],
         out_specs=pl.BlockSpec((1, own, bins, channels), lambda q: (q, 0, 0, 0)),
-    )(packed.reshape(2, channels * 8, 128))
+        scratch_shapes=[pltpu.VMEM((channels * 8, 128), jnp.float32)],
+    )(packed.reshape(2, channels * 8, 128), peaks)
     return spread.transpose(3, 0, 1, 2)
 
 
@@ -322,6 +371,8 @@
             and half % 128 == 0
             and own % 8 == 0
             and (own // 8) * (half // 8) == 128
+            and ng % 2 == 0
+            and ng * chans == 256
         )
         if fits:
             return on_device(nx, ng, voltages, weights)

time: 120 us -> 114 us (0.950)
  the two profiles are of different devices: /device:TPU:25 before, /device:TPU:0 now
where the time goes in v1:
time: 114 us; the launch traced here: 113 us
  Pallas kernels  113 us (99%)
    pallas_call x1, Pallas kernels, on_device(): pl.pallas_call(functools.partial(kernel, nx, ng), out_shape=(jax.ShapeDty...  110 us
    pallas_call x1, Pallas kernels, on_device(): pl.pallas_call(spread_kernel, grid=(2,), out_shape=jax.ShapeDtypeStruct((...  3.34 us

profile of v1, /device:TPU:0, one launch (start us, length us, event | category | flops | bytes accessed | tf_op | source)
XLA Modules:
  0.0 113.4 jit_solution(16758630453557813044)
XLA Ops:
  0.0 110.1 %shard_map.55 = (bf16[2,16,4,32,128]{4,3,2,1,0:T(8,128)(2,1)}, f32[2,8,2,128]{3,2,1,0:T(2,128)}) custom-call(bf16[8,2,256,512]{3,2,1,0:T(8,128)(2,1)} %bitcast.4, bf16[2,16,2,64,512]{4,3,2,1,0:T(8,128)(2,1)} %bitcast.5, bf16[256,256]{1,0:T(8,128)(2,1)} %constant.6.clone.turn_ref, bf16[256,128]{1,0:T(8,128)(2,1)} %constant.7.clone.mix_ref, ...), custom_call_target="tpu_custom_call" | custom-call | tf_op jit(solution)/shard_map/pallas_call | solution.py:314
  110.1 3.3 %shard_map.56 = f32[2,32,32,256]{3,2,1,0:T(8,128)} custom-call(bf16[2,2048,128]{2,1,0:T(8,128)(2,1)} %bitcast.6, f32[2,8,2,128]{3,2,1,0:T(2,128)} %get-tuple-element.8.peak_ref), custom_call_target="tpu_custom_call" | custom-call | tf_op jit(solution)/shard_map/pallas_call | solution.py:346

commit v2 on v1

--- a/solution.py
+++ b/solution.py
@@ -12,9 +12,10 @@
 MESH = pl.DeviceIdType.MESH
 CHUNKS = 4
 PIECES = 4
-LEAD = 2
+LEAD = 6
 TOP = 2.0**15.75
 FLOOR = 2.0**-90
+NEXT = 1.0 + 1.3 / 256
 
 
 def beam_power(voltage, weight_block):
@@ -152,10 +153,12 @@
 
     turn_side(side)
     pl.semaphore_wait(barrier, n - 1)
-    for k in range(LEAD):
+    for k in range(CHUNKS):
         send_voltages(k)
         send_weights(k)
     turn_side(1 - side)
+    for k in range(CHUNKS, LEAD):
+        send_voltages(k)
     w_copy.wait()
 
     def step(k, _):
@@ -164,10 +167,6 @@
         @pl.when(k + LEAD < steps)
         def _():
             send_voltages(k + LEAD)
-
-        @pl.when(k + LEAD < PIECES)
-        def _():
-            send_weights(k + LEAD)
 
         @pl.when((k >= 1) & (k <= PIECES))
         def _():
@@ -212,7 +211,9 @@
         code = work[...].reshape(ng, per * 8, 128) * (TOP / peak)[None]
         code = code * code
         code = code * code
-        pbuf[k] = (code * code).astype(jnp.bfloat16)
+        code = code * code
+        near = code.astype(jnp.bfloat16).astype(jnp.float32)
+        pbuf[k] = jnp.where(code < near, -near, near).astype(jnp.bfloat16)
         row = lax.broadcasted_iota(jnp.int32, peaks.shape, 0)
         lane = lax.broadcasted_iota(jnp.int32, peaks.shape, 1)
         own_row = lax.rem(side + which, 2)
@@ -276,7 +277,11 @@
     channels, bins = out_ref.shape[3], out_ref.shape[2]
     scale = jnp.sum(peak_ref[0], axis=0) * (1.0 / TOP)
     scale = jnp.concatenate([scale[0:1], scale[1:2]], axis=1)
-    power[...] = jnp.exp(jnp.log(in_ref[0].astype(jnp.float32)) * 0.125)
+    code = in_ref[0].astype(jnp.float32)
+    near = jnp.abs(code)
+    gap = (near * NEXT).astype(jnp.bfloat16).astype(jnp.float32) - near
+    near = near + jnp.where(code < 0, -0.25, 0.25) * gap
+    power[...] = jnp.exp(jnp.log(near) * 0.125)
     for r in range(8):
         lanes = power[pl.ds(r, channels, stride=8), :].T * scale
         for m in range(128 // bins):

time: 114 us -> 106 us (0.930)
  Pallas kernels: 113 us -> 106 us
    pallas_call x1, Pallas kernels: 110 us -> 102 us  [on_device(): pl.pallas_call(functools.partial(kernel, nx, ng), out_shape=(jax.ShapeDty...]
where the time goes in v2:
time: 106 us
  Pallas kernels  106 us (100%)
    pallas_call x1, Pallas kernels, on_device(): pl.pallas_call(functools.partial(kernel, nx, ng), out_shape=(jax.ShapeDty...  102 us
    pallas_call x1, Pallas kernels, on_device(): pl.pallas_call(spread_kernel, grid=(2,), out_shape=jax.ShapeDtypeStruct((...  3.79 us

profile of v2, /device:TPU:0, one launch (start us, length us, event | category | flops | bytes accessed | tf_op | source)
XLA Modules:
  0.0 105.9 jit_solution(1733869988653304313)
XLA Ops:
  0.0 102.1 %shard_map.55 = (bf16[2,16,4,32,128]{4,3,2,1,0:T(8,128)(2,1)}, f32[2,8,2,128]{3,2,1,0:T(2,128)}) custom-call(bf16[8,2,256,512]{3,2,1,0:T(8,128)(2,1)} %bitcast.4, bf16[2,16,2,64,512]{4,3,2,1,0:T(8,128)(2,1)} %bitcast.5, bf16[256,256]{1,0:T(8,128)(2,1)} %constant.6.clone.turn_ref, bf16[256,128]{1,0:T(8,128)(2,1)} %constant.7.clone.mix_ref, ...), custom_call_target="tpu_custom_call" | custom-call | tf_op jit(solution)/shard_map/pallas_call | solution.py:319
  102.1 3.8 %shard_map.56 = f32[2,32,32,256]{3,2,1,0:T(8,128)} custom-call(bf16[2,2048,128]{2,1,0:T(8,128)(2,1)} %bitcast.6, f32[2,8,2,128]{3,2,1,0:T(2,128)} %get-tuple-element.8.peak_ref), custom_call_target="tpu_custom_call" | custom-call | tf_op jit(solution)/shard_map/pallas_call | solution.py:351

commit v3 on v2

--- a/solution.py
+++ b/solution.py
@@ -2,16 +2,16 @@
 
 import jax
 import jax.numpy as jnp
-import numpy as np
 from jax import lax
 from jax.experimental import pallas as pl
 from jax.experimental.pallas import tpu as pltpu
 from jax.sharding import PartitionSpec as P
 
-BF16 = np.dtype(jnp.bfloat16)
 MESH = pl.DeviceIdType.MESH
+VMEM = 61 * 1024 * 1024
 CHUNKS = 4
 PIECES = 4
+HOLD = 2
 LEAD = 6
 TOP = 2.0**15.75
 FLOOR = 2.0**-90
@@ -58,17 +58,15 @@
 
 
 def kernel(
-    nx, ng, v_ref, w_hbm, turn_ref, mix_ref, gather_ref, out_ref, peak_ref,
-    sbuf, vrecv, w_ref, work, pbuf, peaks,
-    w_sem, wsend, wz, relay_sem, wx, vsend, vget, psend, pget, msend, mget,
+    nx, ng, v_hbm, w_hbm, out_ref, peak_ref,
+    turn_ref, mix_ref, gather_ref, vbuf, sbuf, vrecv, w_ref, work, pbuf, peaks,
+    v_sem, cross, w_sem, wsend, wz, relay_sem, wx, vsend, vget, psend, pget, msend, mget,
 ):
     x = lax.axis_index("ta")
     g = lax.axis_index("gx")
-    me = x * ng + g
-    n = nx * ng
-    rows = v_ref.shape[0] * v_ref.shape[1]
-    chans = v_ref.shape[2] // ng
-    half = v_ref.shape[3] // nx
+    rows = v_hbm.shape[0] * v_hbm.shape[1]
+    chans = v_hbm.shape[2] // ng
+    half = v_hbm.shape[3] // nx
     per = chans // CHUNKS
     group = ng // 2
     antennas2 = group * rows
@@ -81,26 +79,54 @@
     mine = x * group + u
     piece = chans // nx // PIECES
 
-    w_copy = pltpu.make_async_copy(w_hbm.at[side], w_ref.at[0], w_sem)
-    w_copy.start()
-
     barrier = pltpu.get_barrier_semaphore()
 
     def greet(i, _):
-        d = lax.rem(me + i, n)
+        d = mine ^ i
         pl.semaphore_signal(
-            barrier, inc=1, device_id=(d // ng, lax.rem(d, ng)), device_id_type=MESH
+            barrier,
+            inc=1,
+            device_id=(d // group, side * group + lax.rem(d, group)),
+            device_id_type=MESH,
         )
         return 0
 
-    lax.fori_loop(1, n, greet, 0)
+    lax.fori_loop(1, dests, greet, 0)
+    pl.semaphore_signal(barrier, inc=1, device_id=(x, partner), device_id_type=MESH)
+
+    w_copy = pltpu.make_async_copy(w_hbm.at[side], w_ref.at[0], w_sem)
+
+    def fetch(block):
+        return pltpu.make_async_copy(
+            v_hbm.at[:, :, pl.ds(pl.multiple_of(block * chans, chans), chans), :],
+            vbuf.at[block],
+            v_sem.at[block],
+        )
+
+    def fetch_side(which):
+        def start(i, _):
+            fetch(which * group + i).start()
+            return 0
+
+        lax.fori_loop(0, group, start, 0)
+
+    fetch_side(side)
+    fetch_side(1 - side)
+    w_copy.start()
+
+    def grid_of(shape):
+        return [lax.broadcasted_iota(jnp.int32, shape, axis) for axis in (0, 1)]
+
+    i, j = grid_of(turn_ref.shape)
+    hit = (j % chans == i // rows) & (j // chans == i % rows)
+    turn_ref[...] = hit.astype(jnp.float32).astype(jnp.bfloat16)
 
     def turn_side(which):
         base = lax.rem(which + side, 2) * CHUNKS
 
         def turn(i, _):
-            start = pl.multiple_of((which * group + i) * chans, chans)
-            block = v_ref[:, :, pl.ds(start, chans), :].reshape(rows * chans, nx * half)
+            fetch(which * group + i).wait()
+            block = vbuf[which * group + i].reshape(rows * chans, nx * half)
             turned = jnp.dot(turn_ref[...], block, preferred_element_type=jnp.float32)
             turned = turned.astype(jnp.bfloat16).reshape(CHUNKS, per, rows, nx * half)
             for k in range(nx):
@@ -112,12 +138,18 @@
         lax.fori_loop(0, group, turn, 0)
 
     def send_voltages(k):
-        pltpu.make_async_copy(sbuf.at[k, mine], vrecv.at[k, mine], vget.at[k]).start()
+        first = k // CHUNKS * CHUNKS
+        skew = k // CHUNKS * (CHUNKS // nx)
+
+        def source(d):
+            return sbuf.at[first + lax.rem(k - first + d // group * skew, CHUNKS), d]
+
+        pltpu.make_async_copy(source(mine), vrecv.at[k, mine], vget.at[k]).start()
 
         def send(i, _):
-            d = lax.rem(mine + i, dests)
+            d = mine ^ (dests - i)
             pltpu.make_async_remote_copy(
-                src_ref=sbuf.at[k, d],
+                src_ref=source(d),
                 dst_ref=vrecv.at[k, mine],
                 send_sem=vsend.at[k],
                 recv_sem=vget.at[k],
@@ -146,19 +178,30 @@
             src_ref=block,
             dst_ref=block,
             send_sem=relay_sem,
-            recv_sem=wx,
+            recv_sem=wx.at[i],
             device_id=(1 - x, g),
             device_id_type=MESH,
         ).start()
 
     turn_side(side)
-    pl.semaphore_wait(barrier, n - 1)
+    pl.semaphore_wait(barrier, dests)
+    pl.semaphore_signal(cross, inc=1, device_id=(x, partner), device_id_type=MESH)
     for k in range(CHUNKS):
         send_voltages(k)
         send_weights(k)
     turn_side(1 - side)
     for k in range(CHUNKS, LEAD):
         send_voltages(k)
+    antennas = antennas2 // 2
+    i, j = grid_of(mix_ref.shape)
+    block = i // antennas
+    wants = 2 * (i % antennas) + ((block == 1) | (block == 2)).astype(jnp.int32)
+    sign = jnp.where(block == 1, -1.0, 1.0)
+    mix_ref[...] = jnp.where(j == wants, sign, 0.0).astype(jnp.bfloat16)
+    sample, lane = grid_of(gather_ref.shape[1:])
+    for m in range(gather_ref.shape[0]):
+        hit = lane == m * (half // 8) + sample // 8
+        gather_ref[m] = hit.astype(jnp.float32).astype(jnp.bfloat16)
     w_copy.wait()
 
     def step(k, _):
@@ -168,17 +211,19 @@
         def _():
             send_voltages(k + LEAD)
 
-        @pl.when((k >= 1) & (k <= PIECES))
+        @pl.when((k >= HOLD) & (k < HOLD + PIECES))
         def _():
-            relay_weights(k - 1)
-
-        @pl.when(k == CHUNKS)
-        def _():
-            other = w_ref.at[1, pl.ds((1 - x) * PIECES * piece, PIECES * piece)]
-            pltpu.make_async_copy(other, other, wx).wait()
+            relay_weights(k - HOLD)
+
+        for i in range(PIECES):
+
+            @pl.when(k == steps - CHUNKS // nx + i * CHUNKS // nx // PIECES)
+            def _(i=i):
+                other = w_ref.at[1, pl.ds(((1 - x) * PIECES + i) * piece, piece)]
+                pltpu.make_async_copy(other, other, wx.at[i]).wait()
 
         which = k // CHUNKS
-        part_of = lax.rem(k, CHUNKS)
+        part_of = lax.rem(k + which * x * (CHUNKS // nx), CHUNKS)
 
         def channel(c, peak):
             w = w_ref[which, part_of * per + c].reshape(antennas2, beams).T
@@ -221,11 +266,15 @@
         held = (row == own_row) & (lane >= first) & (lane < first + per)
         peaks[...] = jnp.where(held, peak, peaks[...])
 
+        @pl.when(k == 0)
+        def _():
+            pl.semaphore_wait(cross, 1)
+
         target = out_ref.at[side, lax.rem(g + which * group, ng), part_of]
         pltpu.make_async_copy(pbuf.at[k, g], target, pget).start()
 
         def send(i, _):
-            d = lax.rem(g + i, ng)
+            d = g ^ (ng - i)
             pltpu.make_async_remote_copy(
                 src_ref=pbuf.at[k, d],
                 dst_ref=target,
@@ -300,21 +349,8 @@
     packs = own // 8
     bins = half // 8
 
-    i = np.arange(rows * chans)[:, None]
-    j = np.arange(rows * chans)[None, :]
-    turn = ((j % chans == i // rows) & (j // chans == i % rows)).astype(BF16)
-    i = np.arange(4 * antennas)[:, None]
-    j = np.arange(2 * antennas)[None, :]
-    block = i // antennas
-    wants = 2 * (i % antennas) + np.where((block == 0) | (block == 3), 0, 1)
-    mix = np.where(j == wants, np.where(block == 1, -1.0, 1.0), 0.0).astype(BF16)
-    m = np.arange(packs)[:, None, None]
-    s = np.arange(half)[None, :, None]
-    lane = np.arange(128)[None, None, :]
-    gather = (lane == m * bins + s // 8).astype(BF16)
-
     turned_weights = jnp.swapaxes(weights, 3, 4)
-    vmem = pl.BlockSpec(memory_space=pltpu.VMEM)
+    hbm = pl.BlockSpec(memory_space=pltpu.HBM)
     anywhere = pl.BlockSpec(memory_space=pl.ANY)
     packed, peaks = pl.pallas_call(
         functools.partial(kernel, nx, ng),
@@ -322,20 +358,26 @@
             jax.ShapeDtypeStruct((2, ng, CHUNKS, per * 8, 128), jnp.bfloat16),
             jax.ShapeDtypeStruct((2, group, 2, 128), jnp.float32),
         ),
-        in_specs=[vmem, anywhere, vmem, vmem, vmem],
+        in_specs=[hbm, hbm],
         out_specs=(anywhere, anywhere),
         scratch_shapes=[
+            pltpu.VMEM((rows * chans, rows * chans), jnp.bfloat16),
+            pltpu.VMEM((4 * antennas, 2 * antennas), jnp.bfloat16),
+            pltpu.VMEM((packs, half, 128), jnp.bfloat16),
+            pltpu.VMEM((2 * group, streams, parts, chans, samples), jnp.bfloat16),
             pltpu.VMEM((2 * CHUNKS, nx * group, per, rows, half), jnp.bfloat16),
             pltpu.VMEM((2 * CHUNKS, nx * group, per, rows, half), jnp.bfloat16),
             pltpu.VMEM(turned_weights.shape, jnp.bfloat16),
             pltpu.VMEM((ng, per, 8, 128), jnp.float32),
             pltpu.VMEM((2 * CHUNKS, ng, per * 8, 128), jnp.bfloat16),
             pltpu.VMEM((2, 128), jnp.float32),
+            pltpu.SemaphoreType.DMA((2 * group,)),
+            pltpu.SemaphoreType.REGULAR,
             pltpu.SemaphoreType.DMA,
             pltpu.SemaphoreType.DMA,
             pltpu.SemaphoreType.DMA((PIECES,)),
             pltpu.SemaphoreType.DMA,
-            pltpu.SemaphoreType.DMA,
+            pltpu.SemaphoreType.DMA((PIECES,)),
             pltpu.SemaphoreType.DMA((2 * CHUNKS,)),
             pltpu.SemaphoreType.DMA((2 * CHUNKS,)),
             pltpu.SemaphoreType.DMA,
@@ -344,9 +386,9 @@
             pltpu.SemaphoreType.DMA,
         ],
         compiler_params=pltpu.CompilerParams(
-            collective_id=0, has_side_effects=True, vmem_limit_bytes=56 * 1024 * 1024
+            collective_id=0, has_side_effects=True, vmem_limit_bytes=VMEM
         ),
-    )(v, turned_weights, turn, mix, gather)
+    )(v, turned_weights)
 
     spread = pl.pallas_call(
         spread_kernel,
@@ -358,6 +400,7 @@
         ],
         out_specs=pl.BlockSpec((1, own, bins, channels), lambda q: (q, 0, 0, 0)),
         scratch_shapes=[pltpu.VMEM((channels * 8, 128), jnp.float32)],
+        compiler_params=pltpu.CompilerParams(vmem_limit_bytes=VMEM),
     )(packed.reshape(2, channels * 8, 128), peaks)
     return spread.transpose(3, 0, 1, 2)
 
@@ -377,6 +420,7 @@
             and own % 8 == 0
             and (own // 8) * (half // 8) == 128
             and ng % 2 == 0
+            and ng & (ng - 1) == 0
             and ng * chans == 256
         )
         if fits:

time: 106 us -> 99.1 us (0.935)
  Pallas kernels: 106 us -> 99 us
    pallas_call x1, Pallas kernels: 102 us -> 95.2 us  [on_device(): pl.pallas_call(functools.partial(kernel, nx, ng), out_shape=(jax.ShapeDty...]
where the time goes in v3:
time: 99.1 us; the launch traced here: 99 us
  Pallas kernels  99 us (100%)
    pallas_call x1, Pallas kernels, on_device(): pl.pallas_call(functools.partial(kernel, nx, ng), out_shape=(jax.ShapeDty...  95.2 us
    pallas_call x1, Pallas kernels, on_device(): pl.pallas_call(spread_kernel, grid=(2,), out_shape=jax.ShapeDtypeStruct((...  3.79 us

profile of v3, /device:TPU:0, one launch (start us, length us, event | category | flops | bytes accessed | tf_op | source)
XLA Modules:
  0.0 99.0 jit_solution(2589268136282090424)
XLA Ops:
  0.0 95.2 %shard_map.28 = (bf16[2,16,4,32,128]{4,3,2,1,0:T(8,128)(2,1)}, f32[2,8,2,128]{3,2,1,0:T(2,128)}) custom-call(bf16[8,2,256,512]{3,2,1,0:T(8,128)(2,1)} %bitcast.4, bf16[2,16,2,64,512]{4,3,2,1,0:T(8,128)(2,1)} %bitcast.5), custom_call_target="tpu_custom_call" | custom-call | tf_op jit(solution)/shard_map/pallas_call | solution.py:355
  95.2 3.8 %shard_map.29 = f32[2,32,32,256]{3,2,1,0:T(8,128)} custom-call(bf16[2,2048,128]{2,1,0:T(8,128)(2,1)} %bitcast.6, f32[2,8,2,128]{3,2,1,0:T(2,128)} %get-tuple-element.8.peak_ref), custom_call_target="tpu_custom_call" | custom-call | tf_op jit(solution)/shard_map/pallas_call | solution.py:393

commit v4 on v3

--- a/solution.py
+++ b/solution.py
@@ -8,11 +8,11 @@
 from jax.sharding import PartitionSpec as P
 
 MESH = pl.DeviceIdType.MESH
-VMEM = 61 * 1024 * 1024
+VMEM = 48 * 1024 * 1024
 CHUNKS = 4
 PIECES = 4
 HOLD = 2
-LEAD = 6
+LEAD = 8
 TOP = 2.0**15.75
 FLOOR = 2.0**-90
 NEXT = 1.0 + 1.3 / 256
@@ -59,8 +59,8 @@
 
 def kernel(
     nx, ng, v_hbm, w_hbm, out_ref, peak_ref,
-    turn_ref, mix_ref, gather_ref, vbuf, sbuf, vrecv, w_ref, work, pbuf, peaks,
-    v_sem, cross, w_sem, wsend, wz, relay_sem, wx, vsend, vget, psend, pget, msend, mget,
+    turn_ref, mix_ref, gather_ref, vbuf, sbuf, vrecv, w_ref, work, pbuf, codes, plain, peaks,
+    v_sem, cross, w_sem, wsend, wz, relay_sem, wx, vsend, vget, psend, pget, msend, mget, out_sem,
 ):
     x = lax.axis_index("ta")
     g = lax.axis_index("gx")
@@ -105,7 +105,7 @@
 
     def fetch_side(which):
         def start(i, _):
-            fetch(which * group + i).start()
+            fetch(which * group + (u ^ (group - 1 - i))).start()
             return 0
 
         lax.fori_loop(0, group, start, 0)
@@ -121,41 +121,40 @@
     hit = (j % chans == i // rows) & (j // chans == i % rows)
     turn_ref[...] = hit.astype(jnp.float32).astype(jnp.bfloat16)
 
-    def turn_side(which):
+    def turn_block(which, b):
         base = lax.rem(which + side, 2) * CHUNKS
-
-        def turn(i, _):
-            fetch(which * group + i).wait()
-            block = vbuf[which * group + i].reshape(rows * chans, nx * half)
-            turned = jnp.dot(turn_ref[...], block, preferred_element_type=jnp.float32)
-            turned = turned.astype(jnp.bfloat16).reshape(CHUNKS, per, rows, nx * half)
-            for k in range(nx):
-                sbuf[pl.ds(base, CHUNKS), k * group + i] = turned[
-                    :, :, :, k * half : (k + 1) * half
-                ]
-            return 0
-
-        lax.fori_loop(0, group, turn, 0)
-
-    def send_voltages(k):
+        fetch(which * group + b).wait()
+        block = vbuf[which * group + b].reshape(rows * chans, nx * half)
+        turned = jnp.dot(turn_ref[...], block, preferred_element_type=jnp.float32)
+        turned = turned.astype(jnp.bfloat16).reshape(CHUNKS, per, rows, nx * half)
+        for k in range(nx):
+            sbuf[pl.ds(base, CHUNKS), k * group + b] = turned[
+                :, :, :, k * half : (k + 1) * half
+            ]
+
+    def send_voltage(k, d):
         first = k // CHUNKS * CHUNKS
         skew = k // CHUNKS * (CHUNKS // nx)
-
-        def source(d):
-            return sbuf.at[first + lax.rem(k - first + d // group * skew, CHUNKS), d]
-
-        pltpu.make_async_copy(source(mine), vrecv.at[k, mine], vget.at[k]).start()
+        return pltpu.make_async_remote_copy(
+            src_ref=sbuf.at[first + lax.rem(k - first + d // group * skew, CHUNKS), d],
+            dst_ref=vrecv.at[k, mine],
+            send_sem=vsend.at[k],
+            recv_sem=vget.at[k],
+            device_id=(d // group, side * group + lax.rem(d, group)),
+            device_id_type=MESH,
+        )
+
+    def keep_voltages(k):
+        first = k // CHUNKS * CHUNKS
+        skew = k // CHUNKS * (CHUNKS // nx)
+        own = sbuf.at[first + lax.rem(k - first + x * skew, CHUNKS), mine]
+        pltpu.make_async_copy(own, vrecv.at[k, mine], vget.at[k]).start()
+
+    def send_voltages(k):
+        keep_voltages(k)
 
         def send(i, _):
-            d = mine ^ (dests - i)
-            pltpu.make_async_remote_copy(
-                src_ref=source(d),
-                dst_ref=vrecv.at[k, mine],
-                send_sem=vsend.at[k],
-                recv_sem=vget.at[k],
-                device_id=(d // group, side * group + lax.rem(d, group)),
-                device_id_type=MESH,
-            ).start()
+            send_voltage(k, mine ^ (dests - i)).start()
             return 0
 
         lax.fori_loop(1, dests, send, 0)
@@ -183,13 +182,32 @@
             device_id_type=MESH,
         ).start()
 
-    turn_side(side)
     pl.semaphore_wait(barrier, dests)
     pl.semaphore_signal(cross, inc=1, device_id=(x, partner), device_id_type=MESH)
-    for k in range(CHUNKS):
+
+    def turn_and_send(i, _):
+        @pl.when(i > 0)
+        def _():
+            b = u ^ (group - i)
+            send_voltage(0, (1 - x) * group + b).start()
+            send_voltage(0, x * group + b).start()
+
+        turn_block(side, u ^ (group - 1 - i))
+        return 0
+
+    lax.fori_loop(0, group, turn_and_send, 0)
+    send_weights(0)
+    send_voltage(0, (1 - x) * group + u).start()
+    keep_voltages(0)
+    for k in range(1, CHUNKS):
         send_voltages(k)
         send_weights(k)
-    turn_side(1 - side)
+
+    def turn(i, _):
+        turn_block(1 - side, i)
+        return 0
+
+    lax.fori_loop(0, group, turn, 0)
     for k in range(CHUNKS, LEAD):
         send_voltages(k)
     antennas = antennas2 // 2
@@ -270,8 +288,8 @@
         def _():
             pl.semaphore_wait(cross, 1)
 
-        target = out_ref.at[side, lax.rem(g + which * group, ng), part_of]
-        pltpu.make_async_copy(pbuf.at[k, g], target, pget).start()
+        target = codes.at[side, lax.rem(g + which * group, ng), part_of]
+        pltpu.make_async_copy(pbuf.at[k, g], target, pget.at[k]).start()
 
         def send(i, _):
             d = g ^ (ng - i)
@@ -279,7 +297,7 @@
                 src_ref=pbuf.at[k, d],
                 dst_ref=target,
                 send_sem=psend,
-                recv_sem=pget,
+                recv_sem=pget.at[k],
                 device_id=(x, d),
                 device_id_type=MESH,
             ).start()
@@ -306,8 +324,27 @@
 
     lax.fori_loop(1, ng, send_peaks, 0)
 
+    def decode(k, _):
+        pltpu.make_async_copy(pbuf.at[k], pbuf.at[k], pget.at[k]).wait()
+        which = k // CHUNKS
+        part_of = lax.rem(k + which * x * (CHUNKS // nx), CHUNKS)
+        for other in range(2):
+            span = pl.ds((other + which) % 2 * group, group)
+            code = codes[other, span, part_of].astype(jnp.float32)
+            near = jnp.abs(code)
+            gap = (near * NEXT).astype(jnp.bfloat16).astype(jnp.float32) - near
+            near = near + jnp.where(code < 0, -0.25, 0.25) * gap
+            plain[other, span, part_of] = jnp.exp(jnp.log(near) * 0.125)
+            pltpu.make_async_copy(
+                plain.at[other, span, part_of],
+                out_ref.at[other, span, part_of],
+                out_sem,
+            ).start()
+        return 0
+
+    lax.fori_loop(0, steps, decode, 0)
     pltpu.make_async_copy(peak_ref, peak_ref, mget).wait()
-    pltpu.make_async_copy(out_ref, out_ref, pget).wait()
+    pltpu.make_async_copy(out_ref, out_ref, out_sem).wait()
     for k in range(steps):
         sent = sbuf.at[k, pl.ds(0, dests - 1)]
         pltpu.make_async_copy(sent, sent, vsend.at[k]).wait()
@@ -322,17 +359,12 @@
     pltpu.make_async_copy(sent, sent, relay_sem).wait()
 
 
-def spread_kernel(in_ref, peak_ref, out_ref, power):
+def spread_kernel(in_ref, peak_ref, out_ref):
     channels, bins = out_ref.shape[3], out_ref.shape[2]
     scale = jnp.sum(peak_ref[0], axis=0) * (1.0 / TOP)
     scale = jnp.concatenate([scale[0:1], scale[1:2]], axis=1)
-    code = in_ref[0].astype(jnp.float32)
-    near = jnp.abs(code)
-    gap = (near * NEXT).astype(jnp.bfloat16).astype(jnp.float32) - near
-    near = near + jnp.where(code < 0, -0.25, 0.25) * gap
-    power[...] = jnp.exp(jnp.log(near) * 0.125)
     for r in range(8):
-        lanes = power[pl.ds(r, channels, stride=8), :].T * scale
+        lanes = in_ref[0, pl.ds(r, channels, stride=8), :].T * scale
         for m in range(128 // bins):
             out_ref[0, m * 8 + r] = lanes[m * bins : (m + 1) * bins]
 
@@ -355,7 +387,7 @@
     packed, peaks = pl.pallas_call(
         functools.partial(kernel, nx, ng),
         out_shape=(
-            jax.ShapeDtypeStruct((2, ng, CHUNKS, per * 8, 128), jnp.bfloat16),
+            jax.ShapeDtypeStruct((2, ng, CHUNKS, per * 8, 128), jnp.float32),
             jax.ShapeDtypeStruct((2, group, 2, 128), jnp.float32),
         ),
         in_specs=[hbm, hbm],
@@ -370,6 +402,8 @@
             pltpu.VMEM(turned_weights.shape, jnp.bfloat16),
             pltpu.VMEM((ng, per, 8, 128), jnp.float32),
             pltpu.VMEM((2 * CHUNKS, ng, per * 8, 128), jnp.bfloat16),
+            pltpu.VMEM((2, ng, CHUNKS, per * 8, 128), jnp.bfloat16),
+            pltpu.VMEM((2, ng, CHUNKS, per * 8, 128), jnp.float32),
             pltpu.VMEM((2, 128), jnp.float32),
             pltpu.SemaphoreType.DMA((2 * group,)),
             pltpu.SemaphoreType.REGULAR,
@@ -381,6 +415,7 @@
             pltpu.SemaphoreType.DMA((2 * CHUNKS,)),
             pltpu.SemaphoreType.DMA((2 * CHUNKS,)),
             pltpu.SemaphoreType.DMA,
+            pltpu.SemaphoreType.DMA((2 * CHUNKS,)),
             pltpu.SemaphoreType.DMA,
             pltpu.SemaphoreType.DMA,
             pltpu.SemaphoreType.DMA,
@@ -399,7 +434,6 @@
             pl.BlockSpec((1, group, 2, 128), lambda q: (q, 0, 0, 0)),
         ],
         out_specs=pl.BlockSpec((1, own, bins, channels), lambda q: (q, 0, 0, 0)),
-        scratch_shapes=[pltpu.VMEM((channels * 8, 128), jnp.float32)],
         compiler_params=pltpu.CompilerParams(vmem_limit_bytes=VMEM),
     )(packed.reshape(2, channels * 8, 128), peaks)
     return spread.transpose(3, 0, 1, 2)

time: 99.1 us -> 96 us (0.969)
  Pallas kernels: 99 us -> 95.8 us
    pallas_call x1, Pallas kernels: 3.79 us -> 1.69 us  [on_device(): pl.pallas_call(spread_kernel, grid=(2,), out_shape=jax.ShapeDtypeStruct((...]
    pallas_call x1, Pallas kernels: 95.2 us -> 94.1 us  [on_device(): pl.pallas_call(functools.partial(kernel, nx, ng), out_shape=(jax.ShapeDty...]
where the time goes in v4:
time: 96 us; the launch traced here: 95.8 us
  Pallas kernels  95.8 us (100%)
    pallas_call x1, Pallas kernels, on_device(): pl.pallas_call(functools.partial(kernel, nx, ng), out_shape=(jax.ShapeDty...  94.1 us

profile of v4, /device:TPU:0, one launch (start us, length us, event | category | flops | bytes accessed | tf_op | source)
XLA Modules:
  0.0 95.8 jit_solution(17440439447576573304)
XLA Ops:
  0.0 94.1 %shard_map.28 = (f32[2,16,4,32,128]{4,3,2,1,0:T(8,128)S(1)}, f32[2,8,2,128]{3,2,1,0:T(2,128)S(1)}) custom-call(bf16[8,2,256,512]{3,2,1,0:T(8,128)(2,1)} %bitcast.5, bf16[2,16,2,64,512]{4,3,2,1,0:T(8,128)(2,1)} %bitcast.6), custom_call_target="tpu_custom_call" | custom-call | tf_op jit(solution)/shard_map/pallas_call | solution.py:387
  94.1 1.7 %shard_map.29 = f32[2,32,32,256]{3,2,1,0:T(8,128)} custom-call(f32[2,2048,128]{2,1,0:T(8,128)S(1)} %bitcast.4, f32[2,8,2,128]{3,2,1,0:T(2,128)S(1)} %get-tuple-element.8.peak_ref), custom_call_target="tpu_custom_call" | custom-call | tf_op jit(solution)/shard_map/pallas_call | solution.py:428

commit v5 on v4

--- a/solution.py
+++ b/solution.py
@@ -13,6 +13,7 @@
 PIECES = 4
 HOLD = 2
 LEAD = 8
+NEAR = 2
 TOP = 2.0**15.75
 FLOOR = 2.0**-90
 NEXT = 1.0 + 1.3 / 256
@@ -221,6 +222,30 @@
         hit = lane == m * (half // 8) + sample // 8
         gather_ref[m] = hit.astype(jnp.float32).astype(jnp.bfloat16)
     w_copy.wait()
+
+    def power_slot(k):
+        which = k // CHUNKS
+        part_of = lax.rem(k + which * x * (CHUNKS // nx), CHUNKS)
+        return codes.at[side, lax.rem(g + which * group, ng), part_of]
+
+    def send_powers(k, d):
+        pltpu.make_async_remote_copy(
+            src_ref=pbuf.at[k, d],
+            dst_ref=power_slot(k),
+            send_sem=psend,
+            recv_sem=pget.at[k],
+            device_id=(x, d),
+            device_id_type=MESH,
+        ).start()
+
+    def send_near(k):
+        pltpu.make_async_copy(pbuf.at[k, g], power_slot(k), pget.at[k]).start()
+
+        def send(i, _):
+            send_powers(k, g ^ (group - i))
+            return 0
+
+        lax.fori_loop(1, group, send, 0)
 
     def step(k, _):
         pltpu.make_async_copy(vrecv.at[k], vrecv.at[k], vget.at[k]).wait()
@@ -288,22 +313,20 @@
         def _():
             pl.semaphore_wait(cross, 1)
 
-        target = codes.at[side, lax.rem(g + which * group, ng), part_of]
-        pltpu.make_async_copy(pbuf.at[k, g], target, pget.at[k]).start()
-
         def send(i, _):
-            d = g ^ (ng - i)
-            pltpu.make_async_remote_copy(
-                src_ref=pbuf.at[k, d],
-                dst_ref=target,
-                send_sem=psend,
-                recv_sem=pget.at[k],
-                device_id=(x, d),
-                device_id_type=MESH,
-            ).start()
+            send_powers(k, (1 - side) * group + i)
             return 0
 
-        lax.fori_loop(1, ng, send, 0)
+        lax.fori_loop(0, group, send, 0)
+
+        @pl.when(side == 0)
+        def _():
+            send_near(k)
+
+        @pl.when((side == 1) & (k >= NEAR))
+        def _():
+            send_near(k - NEAR)
+
         return 0
 
     peaks[...] = jnp.zeros_like(peaks)
@@ -323,6 +346,14 @@
         return 0
 
     lax.fori_loop(1, ng, send_peaks, 0)
+
+    @pl.when(side == 1)
+    def _():
+        def late(k, _):
+            send_near(k)
+            return 0
+
+        lax.fori_loop(steps - NEAR, steps, late, 0)
 
     def decode(k, _):
         pltpu.make_async_copy(pbuf.at[k], pbuf.at[k], pget.at[k]).wait()

time: 96 us -> 95.5 us (level)
  no operation moved by 1% of the time
where the time goes in v5:
time: 95.5 us; the launch traced here: 95.3 us
  Pallas kernels  95.3 us (100%)
    pallas_call x1, Pallas kernels, on_device(): pl.pallas_call(functools.partial(kernel, nx, ng), out_shape=(jax.ShapeDty...  93.6 us

profile of v5, /device:TPU:0, one launch (start us, length us, event | category | flops | bytes accessed | tf_op | source)
XLA Modules:
  0.0 95.3 jit_solution(4158139353867296026)
XLA Ops:
  0.0 93.6 %shard_map.28 = (f32[2,16,4,32,128]{4,3,2,1,0:T(8,128)S(1)}, f32[2,8,2,128]{3,2,1,0:T(2,128)S(1)}) custom-call(bf16[8,2,256,512]{3,2,1,0:T(8,128)(2,1)} %bitcast.5, bf16[2,16,2,64,512]{4,3,2,1,0:T(8,128)(2,1)} %bitcast.6), custom_call_target="tpu_custom_call" | custom-call | tf_op jit(solution)/shard_map/pallas_call | solution.py:418
  93.6 1.7 %shard_map.29 = f32[2,32,32,256]{3,2,1,0:T(8,128)} custom-call(f32[2,2048,128]{2,1,0:T(8,128)S(1)} %bitcast.4, f32[2,8,2,128]{3,2,1,0:T(2,128)S(1)} %get-tuple-element.8.peak_ref), custom_call_target="tpu_custom_call" | custom-call | tf_op jit(solution)/shard_map/pallas_call | solution.py:459

commit v6 on v5

--- a/solution.py
+++ b/solution.py
@@ -13,7 +13,7 @@
 PIECES = 4
 HOLD = 2
 LEAD = 8
-NEAR = 2
+NEAR = 3
 TOP = 2.0**15.75
 FLOOR = 2.0**-90
 NEXT = 1.0 + 1.3 / 256
@@ -75,6 +75,7 @@
     side = g // group
     u = lax.rem(g, group)
     partner = lax.rem(g + group, ng)
+    last = (side == 1) & (u >= group // 2)
     steps = 2 * CHUNKS
     dests = nx * group
     mine = x * group + u
@@ -186,6 +187,8 @@
     pl.semaphore_wait(barrier, dests)
     pl.semaphore_signal(cross, inc=1, device_id=(x, partner), device_id_type=MESH)
 
+    send_weights(0)
+
     def turn_and_send(i, _):
         @pl.when(i > 0)
         def _():
@@ -197,7 +200,6 @@
         return 0
 
     lax.fori_loop(0, group, turn_and_send, 0)
-    send_weights(0)
     send_voltage(0, (1 - x) * group + u).start()
     keep_voltages(0)
     for k in range(1, CHUNKS):
@@ -317,13 +319,17 @@
             send_powers(k, (1 - side) * group + i)
             return 0
 
+        @pl.when(side == 0)
+        def _():
+            send_near(k)
+
         lax.fori_loop(0, group, send, 0)
 
-        @pl.when(side == 0)
+        @pl.when(~last & (side == 1))
         def _():
             send_near(k)
 
-        @pl.when((side == 1) & (k >= NEAR))
+        @pl.when(last & (k >= NEAR))
         def _():
             send_near(k - NEAR)
 
@@ -347,7 +353,7 @@
 
     lax.fori_loop(1, ng, send_peaks, 0)
 
-    @pl.when(side == 1)
+    @pl.when(last)
     def _():
         def late(k, _):
             send_near(k)
@@ -390,14 +396,29 @@
     pltpu.make_async_copy(sent, sent, relay_sem).wait()
 
 
-def spread_kernel(in_ref, peak_ref, out_ref):
+def spread_kernel(in_ref, peak_ref, out_ref, block, sem):
     channels, bins = out_ref.shape[3], out_ref.shape[2]
-    scale = jnp.sum(peak_ref[0], axis=0) * (1.0 / TOP)
-    scale = jnp.concatenate([scale[0:1], scale[1:2]], axis=1)
-    for r in range(8):
-        lanes = in_ref[0, pl.ds(r, channels, stride=8), :].T * scale
-        for m in range(128 // bins):
-            out_ref[0, m * 8 + r] = lanes[m * bins : (m + 1) * bins]
+    packs = 128 // bins
+
+    def copies(q, r):
+        for m in range(packs):
+            yield pltpu.make_async_copy(block.at[q, m * 8 + r], out_ref.at[q, m * 8 + r], sem)
+
+    before = None
+    for q in range(2):
+        scale = jnp.sum(peak_ref[q], axis=0) * (1.0 / TOP)
+        scale = jnp.concatenate([scale[0:1], scale[1:2]], axis=1)
+        for r in range(8):
+            lanes = in_ref[q, pl.ds(r, channels, stride=8), :].T * scale
+            for m in range(packs):
+                block[q, m * 8 + r] = lanes[m * bins : (m + 1) * bins]
+            if before is not None:
+                for copy in copies(*before):
+                    copy.start()
+            before = (q, r)
+    for copy in copies(*before):
+        copy.start()
+    pltpu.make_async_copy(block, out_ref, sem).wait()
 
 
 def on_device(nx, ng, voltages, weights):
@@ -458,13 +479,13 @@
 
     spread = pl.pallas_call(
         spread_kernel,
-        grid=(2,),
         out_shape=jax.ShapeDtypeStruct((2, own, bins, channels), jnp.float32),
-        in_specs=[
-            pl.BlockSpec((1, channels * 8, 128), lambda q: (q, 0, 0)),
-            pl.BlockSpec((1, group, 2, 128), lambda q: (q, 0, 0, 0)),
+        in_specs=[pl.BlockSpec(memory_space=pltpu.VMEM)] * 2,
+        out_specs=anywhere,
+        scratch_shapes=[
+            pltpu.VMEM((2, own, bins, channels), jnp.float32),
+            pltpu.SemaphoreType.DMA,
         ],
-        out_specs=pl.BlockSpec((1, own, bins, channels), lambda q: (q, 0, 0, 0)),
         compiler_params=pltpu.CompilerParams(vmem_limit_bytes=VMEM),
     )(packed.reshape(2, channels * 8, 128), peaks)
     return spread.transpose(3, 0, 1, 2)

time: 95.5 us -> 94.6 us (level)
  no operation moved by 1% of the time
where the time goes in v6:
time: 94.6 us; the launch traced here: 94.5 us
  Pallas kernels  94.4 us (100%)
    pallas_call x1, Pallas kernels, on_device(): pl.pallas_call(functools.partial(kernel, nx, ng), out_shape=(jax.ShapeDty...  93 us

profile of v6, /device:TPU:0, one launch (start us, length us, event | category | flops | bytes accessed | tf_op | source)
XLA Modules:
  0.0 94.5 jit_solution(12805530891820196586)
XLA Ops:
  0.0 93.0 %shard_map.28 = (f32[2,16,4,32,128]{4,3,2,1,0:T(8,128)S(1)}, f32[2,8,2,128]{3,2,1,0:T(2,128)S(1)}) custom-call(bf16[8,2,256,512]{3,2,1,0:T(8,128)(2,1)} %bitcast.5, bf16[2,16,2,64,512]{4,3,2,1,0:T(8,128)(2,1)} %bitcast.6), custom_call_target="tpu_custom_call" | custom-call | tf_op jit(solution)/shard_map/pallas_call | solution.py:439
  93.0 1.4 %shard_map.29 = f32[2,32,32,256]{3,2,1,0:T(8,128)} custom-call(f32[2,2048,128]{2,1,0:T(8,128)S(1)} %bitcast.4, f32[2,8,2,128]{3,2,1,0:T(2,128)S(1)} %get-tuple-element.8.peak_ref), custom_call_target="tpu_custom_call" | custom-call | tf_op jit(solution)/shard_map/pallas_call | solution.py:480

commit v7 on v6

--- a/solution.py
+++ b/solution.py
@@ -9,11 +9,11 @@
 
 MESH = pl.DeviceIdType.MESH
 VMEM = 48 * 1024 * 1024
-CHUNKS = 4
+CHUNKS = 8
 PIECES = 4
 HOLD = 2
-LEAD = 8
-NEAR = 3
+LEAD = 16
+NEAR = 6
 TOP = 2.0**15.75
 FLOOR = 2.0**-90
 NEXT = 1.0 + 1.3 / 256
@@ -204,7 +204,8 @@
     keep_voltages(0)
     for k in range(1, CHUNKS):
         send_voltages(k)
-        send_weights(k)
+        if k % (CHUNKS // PIECES) == 0:
+            send_weights(k // (CHUNKS // PIECES))
 
     def turn(i, _):
         turn_block(1 - side, i)

time: 94.6 us -> 94.2 us (level)
  no operation moved by 1% of the time
where the time goes in v7:
time: 94.2 us; the launch traced here: 94.1 us
  Pallas kernels  94 us (100%)
    pallas_call x1, Pallas kernels, on_device(): pl.pallas_call(functools.partial(kernel, nx, ng), out_shape=(jax.ShapeDty...  92.6 us

profile of v7, /device:TPU:0, one launch (start us, length us, event | category | flops | bytes accessed | tf_op | source)
XLA Modules:
  0.0 94.1 jit_solution(8871838534830319274)
XLA Ops:
  0.0 92.6 %shard_map.28 = (f32[2,16,8,16,128]{4,3,2,1,0:T(8,128)S(1)}, f32[2,8,2,128]{3,2,1,0:T(2,128)S(1)}) custom-call(bf16[8,2,256,512]{3,2,1,0:T(8,128)(2,1)} %bitcast.5, bf16[2,16,2,64,512]{4,3,2,1,0:T(8,128)(2,1)} %bitcast.6), custom_call_target="tpu_custom_call" | custom-call | tf_op jit(solution)/shard_map/pallas_call | solution.py:440
  92.6 1.4 %shard_map.29 = f32[2,32,32,256]{3,2,1,0:T(8,128)} custom-call(f32[2,2048,128]{2,1,0:T(8,128)S(1)} %bitcast.4, f32[2,8,2,128]{3,2,1,0:T(2,128)S(1)} %get-tuple-element.8.peak_ref), custom_call_target="tpu_custom_call" | custom-call | tf_op jit(solution)/shard_map/pallas_call | solution.py:481

commit v8 on v7

--- a/solution.py
+++ b/solution.py
@@ -113,8 +113,6 @@
         lax.fori_loop(0, group, start, 0)
 
     fetch_side(side)
-    fetch_side(1 - side)
-    w_copy.start()
 
     def grid_of(shape):
         return [lax.broadcasted_iota(jnp.int32, shape, axis) for axis in (0, 1)]
@@ -200,6 +198,8 @@
         return 0
 
     lax.fori_loop(0, group, turn_and_send, 0)
+    fetch_side(1 - side)
+    w_copy.start()
     send_voltage(0, (1 - x) * group + u).start()
     keep_voltages(0)
     for k in range(1, CHUNKS):

time: 94.2 us -> 94.2 us (level)
  no operation moved by 1% of the time
where the time goes in v8:
time: 94.2 us; the launch traced here: 94.1 us
  Pallas kernels  94 us (100%)
    pallas_call x1, Pallas kernels, on_device(): pl.pallas_call(functools.partial(kernel, nx, ng), out_shape=(jax.ShapeDty...  92.6 us

profile of v8, /device:TPU:0, one launch (start us, length us, event | category | flops | bytes accessed | tf_op | source)
XLA Modules:
  0.0 94.1 jit_solution(17772715773762432092)
XLA Ops:
  0.0 92.6 %shard_map.28 = (f32[2,16,8,16,128]{4,3,2,1,0:T(8,128)S(1)}, f32[2,8,2,128]{3,2,1,0:T(2,128)S(1)}) custom-call(bf16[8,2,256,512]{3,2,1,0:T(8,128)(2,1)} %bitcast.5, bf16[2,16,2,64,512]{4,3,2,1,0:T(8,128)(2,1)} %bitcast.6), custom_call_target="tpu_custom_call" | custom-call | tf_op jit(solution)/shard_map/pallas_call | solution.py:440
  92.6 1.4 %shard_map.29 = f32[2,32,32,256]{3,2,1,0:T(8,128)} custom-call(f32[2,2048,128]{2,1,0:T(8,128)S(1)} %bitcast.4, f32[2,8,2,128]{3,2,1,0:T(2,128)S(1)} %get-tuple-element.8.peak_ref), custom_call_target="tpu_custom_call" | custom-call | tf_op jit(solution)/shard_map/pallas_call | solution.py:481

commit v9 on v8

--- a/solution.py
+++ b/solution.py
@@ -117,9 +117,6 @@
     def grid_of(shape):
         return [lax.broadcasted_iota(jnp.int32, shape, axis) for axis in (0, 1)]
 
-    i, j = grid_of(turn_ref.shape)
-    hit = (j % chans == i // rows) & (j // chans == i % rows)
-    turn_ref[...] = hit.astype(jnp.float32).astype(jnp.bfloat16)
 
     def turn_block(which, b):
         base = lax.rem(which + side, 2) * CHUNKS
@@ -186,6 +183,9 @@
     pl.semaphore_signal(cross, inc=1, device_id=(x, partner), device_id_type=MESH)
 
     send_weights(0)
+    i, j = grid_of(turn_ref.shape)
+    hit = (j % chans == i // rows) & (j // chans == i % rows)
+    turn_ref[...] = hit.astype(jnp.float32).astype(jnp.bfloat16)
 
     def turn_and_send(i, _):
         @pl.when(i > 0)

time: 94.2 us -> 94.3 us (level)
  no operation moved by 1% of the time
where the time goes in v9:
time: 94.3 us; the launch traced here: 94.1 us
  Pallas kernels  94.1 us (100%)
    pallas_call x1, Pallas kernels, on_device(): pl.pallas_call(functools.partial(kernel, nx, ng), out_shape=(jax.ShapeDty...  92.7 us

profile of v9, /device:TPU:0, one launch (start us, length us, event | category | flops | bytes accessed | tf_op | source)
XLA Modules:
  0.0 94.1 jit_solution(15580308646718577493)
XLA Ops:
  0.0 92.7 %shard_map.28 = (f32[2,16,8,16,128]{4,3,2,1,0:T(8,128)S(1)}, f32[2,8,2,128]{3,2,1,0:T(2,128)S(1)}) custom-call(bf16[8,2,256,512]{3,2,1,0:T(8,128)(2,1)} %bitcast.5, bf16[2,16,2,64,512]{4,3,2,1,0:T(8,128)(2,1)} %bitcast.6), custom_call_target="tpu_custom_call" | custom-call | tf_op jit(solution)/shard_map/pallas_call | solution.py:440
  92.7 1.4 %shard_map.29 = f32[2,32,32,256]{3,2,1,0:T(8,128)} custom-call(f32[2,2048,128]{2,1,0:T(8,128)S(1)} %bitcast.4, f32[2,8,2,128]{3,2,1,0:T(2,128)S(1)} %get-tuple-element.8.peak_ref), custom_call_target="tpu_custom_call" | custom-call | tf_op jit(solution)/shard_map/pallas_call | solution.py:481
